TPU v7x, 128 devices: a whole 4x4x4 slice. The times are simulated.
128 devices in a mesh: row: 16 (over x, y_lo, core), col: 8 (over y_hi, z).
Axes of the slice: x: 4, y: 4 (y_hi: 2, y_lo: 2; y = y_hi * 2 + y_lo), z: 4, core: 2. Of those that a mesh axis runs over, the one named last changes fastest.
Arguments:
- vectors: bfloat16 [64, 1024, 512], P('col', 'row'), may hold values from -6 to 6
- right_factors: bfloat16 [64, 64, 1024, 128], P('row', 'col'), may hold values from -0.1875 to 0.1875
- left_factors: bfloat16 [64, 64, 1024, 128], P('row', 'col'), may hold values from -0.09375 to 0.09375
- tile_ranks: int32 [64, 64], P('row', 'col'), may hold values from 16 to 128
- owner_map: int32 [64], replicated, may hold values from 0 to 63, as said below
Outputs:
- applied: bfloat16 [64, 1024, 512], P('row', 'col')
Inputs may be any that keep to these rules, and one draw needn't show every extreme that they name: owner_map is a permutation of 0 to 63; the 4 stored tile rows held by index i of row (stored rows i * 4 to i * 4 + 3) belong to 4 different indices of row of applied, i + c mod 16 for the same 4 offsets c at every i.
All inputs are finite; a program needn't handle non-finite values.
Results may differ from a plain program's by a relative error of at most 0.0066.
Values may be sent and summed in bfloat16 or wider, within the bound.
A program may use at most 128 MiB of HBM per device.

v0:
```python
import jax
import jax.numpy as jnp
from jax import lax
from jax.sharding import PartitionSpec as P


def split_up(x, dim, peers):
    before, after = (x.shape[:dim], x.shape[dim + 1 :])
    return jnp.moveaxis(x.reshape(*before, peers, -1, *after), dim, 0)


def sent_and_summed(x, axis, dim):
    pieces = split_up(x, dim, lax.axis_size(axis))
    arrived = lax.all_to_all(pieces, axis, split_axis=0, concat_axis=0, tiled=True)
    return arrived.astype(jnp.float32).sum(axis=0)


def masked_coeffs(products, tile_ranks, rank_width):
    columns = jnp.arange(rank_width, dtype=jnp.int32)
    kept_mask = columns[None, None, :] < tile_ranks[:, :, None]
    return jnp.where(kept_mask[:, :, :, None], products, 0.0).astype(jnp.bfloat16)


def build_buffer(payload, owner_map, cycle_size):
    held_rows = payload.shape[0]
    own_rows = lax.dynamic_slice_in_dim(owner_map, lax.axis_index("row") * held_rows, held_rows)
    target = own_rows // held_rows
    devices = jnp.arange(cycle_size, dtype=jnp.int32)
    matches = target[None, :] == devices[:, None]
    present = jnp.any(matches, axis=1)
    source_slot = jnp.sum(
        jnp.where(matches, jnp.arange(held_rows, dtype=jnp.int32)[None, :], 0), axis=1
    )
    picked = jnp.take(payload, source_slot, axis=0)
    return jnp.where(present[:, None, None], picked, jnp.zeros_like(picked))


def pick_rows(received, owner_map, held_rows):
    wanted = lax.axis_index("row") * held_rows + jnp.arange(held_rows, dtype=jnp.int32)
    matches = owner_map[None, :] == wanted[:, None]
    anchor = jnp.sum(
        jnp.where(matches, jnp.arange(owner_map.shape[0], dtype=jnp.int32)[None, :], 0), axis=1
    )
    return jnp.take(received, anchor // held_rows, axis=0)


def on_device(vectors, right_factors, left_factors, tile_ranks, owner_map):
    held_rows = right_factors.shape[0]
    rank_width = right_factors.shape[3]
    cycle_size = lax.axis_size("row")
    products = jnp.einsum(
        "ikbr,kbv->ikrv",
        right_factors,
        lax.all_gather(vectors, "row", axis=1, tiled=True),
        preferred_element_type=jnp.float32,
    )
    coeffs = masked_coeffs(products, tile_ranks, rank_width)
    partial_rows = jnp.einsum(
        "ikbr,ikrv->ibv", left_factors, coeffs, preferred_element_type=jnp.float32
    )
    summed = sent_and_summed(partial_rows.astype(jnp.bfloat16), "col", 1).astype(jnp.bfloat16)
    buffer = build_buffer(summed, owner_map, cycle_size)
    received = lax.all_to_all(buffer, "row", split_axis=0, concat_axis=0, tiled=True)
    applied = pick_rows(received, owner_map, held_rows)
    return applied


def solution(mesh):
    placed = (
        P("col", "row", None),
        P("row", "col", None, None),
        P("row", "col", None, None),
        P("row", "col"),
        P(),
    )
    return jax.shard_map(
        on_device, mesh=mesh, in_specs=placed, out_specs=P("row", "col", None), check_vma=False
    )
```

profile of v0, /device:TPU:25, one launch (start us, length us, event | category | flops | bytes accessed | tf_op | source)
XLA Modules:
  0.0 188.2 jit_solution(1948998117102520125)
XLA Ops:
  6.5 0.0 all-gather.2.cloned.1.call-start
  6.5 0.7 all-gather.2.cloned.1.call-update
  7.3 0.8 iota_compare_fusion
  8.0 55.5 %all-gather.2.cloned.1.call-done = bf16[8,1024,512]{2,1,0:T(8,128)(2,1)} async-done(((bf16[8,64,512]{2,1,0:T(8,128)(2,1)}), bf16[8,1024,512]{2,1,0:T(8,128)(2,1)}) %all-gather.2.cloned.1.call-update) | async-done | bytes 8388624 | tf_op jit(solution)/shard_map/all_gather | solution.py:54
  63.5 16.4 %fusion.5 = bf16[4,64,8,8,128]{4,3,2,1,0:T(8,128)(2,1)} fusion(bf16[4,8,1024,128]{3,2,1,0:T(8,128)(2,1)} %param.7, pred[4,8,128]{2,1,0:T(8,128)(4,1)S(1)} %iota_compare_fusion, bf16[4,8,1024,128]{3,2,1,0:T(8,128)(2,1)} %param.6, bf16[8,1024,512]{2,1,0:T(8,128)(2,1)} %all-gather.2.cloned.1.call-done), kind=kOutput, calls=%fused_computation.8 | convolution fusion | flops 8596226048 | bytes 29364224 | tf_op jit(solution)/shard_map/ikbr,ikrv->ibv/dot_general | solution.py:58
  79.9 5.3 %copy.18 = bf16[4,64,8,8,128]{4,3,1,0,2:T(8,128)(2,1)} copy(bf16[4,64,8,8,128]{4,3,2,1,0:T(8,128)(2,1)} %fusion.5) | data formatting | bytes 8388608 | tf_op jit(solution)/shard_map/reshape | solution.py:9
  85.2 0.0 copy-start
  85.2 7.0 %all-to-all-start = ((bf16[8,4,128,512]{2,3,1,0:T(8,128)(2,1)}), bf16[8,4,128,512]{2,3,1,0:T(8,128)(2,1)}, u32[]{:S(2)}, u32[]{:S(2)}) async-start(bf16[8,4,128,512]{2,3,1,0:T(8,128)(2,1)} %bitcast.48), calls=%async_computation | async-start | bytes 8388608 | tf_op jit(solution)/shard_map/all_to_all | solution.py:14
  92.1 0.0 copy-done
  92.1 0.1 and_select_fusion.1
  92.2 0.1 select_reduce_fusion
  92.3 0.1 fusion.16
  92.4 48.2 %all-to-all-done = bf16[8,4,128,512]{2,3,1,0:T(8,128)(2,1)} async-done(((bf16[8,4,128,512]{2,3,1,0:T(8,128)(2,1)}), bf16[8,4,128,512]{2,3,1,0:T(8,128)(2,1)}, u32[]{:S(2)}, u32[]{:S(2)}) %all-to-all-start) | async-done | bytes 4194336 | tf_op jit(solution)/shard_map/all_to_all | solution.py:14
  140.6 2.9 %reduce_sum.36 = bf16[4,128,512]{1,2,0:T(8,128)(2,1)S(1)} reduce(bf16[8,4,128,512]{2,3,1,0:T(8,128)(2,1)} %all-to-all-done, bf16[]{:T(256)} %constant.65.clone.1), dimensions={0}, to_apply=%region_3.4 | reduce | flops 1835008 | bytes 4718594 | tf_op jit(solution)/shard_map/reduce_sum | solution.py:15
  143.5 0.2 copy.13
  143.7 0.7 gather_fusion
  144.4 1.7 select_select_fusion
  146.1 5.8 %all-to-all-start.1 = ((bf16[16,128,512]{2,1,0:T(8,128)(2,1)}), bf16[16,128,512]{2,1,0:T(8,128)(2,1)S(1)}, u32[]{:S(2)}, u32[]{:S(2)}) async-start(bf16[16,128,512]{2,1,0:T(8,128)(2,1)} %select_select_fusion), calls=%async_computation.1 | async-start | bytes 4194304 | tf_op jit(solution)/shard_map/all_to_all | solution.py:63
  151.9 0.2 select_reduce_fusion.1
  152.1 27.7 %all-to-all-done.1 = bf16[16,128,512]{2,1,0:T(8,128)(2,1)S(1)} async-done(((bf16[16,128,512]{2,1,0:T(8,128)(2,1)}), bf16[16,128,512]{2,1,0:T(8,128)(2,1)S(1)}, u32[]{:S(2)}, u32[]{:S(2)}) %all-to-all-start.1) | async-done | bytes 2097184 | tf_op jit(solution)/shard_map/all_to_all | solution.py:63
  179.8 0.6 gather_fusion.1
  180.4 0.9 broadcast_select_fusion
  (7 shorter events, 0.1 us)
Async XLA Ops:
  6.5 57.0 %all-gather.2.cloned.1.call-start = ((), (), s32[]{:S(2)}) async-start(), calls=%async_computation.2 | async-start | bytes 8912896 | tf_op jit(solution)/shard_map/all_gather | solution.py:54
  85.2 7.0 %copy-start = (s32[64]{0:T(128)S(1)}, s32[64]{0:T(128)}, u32[]{:S(2)}) copy-start(s32[64]{0:T(128)} %param.9) | copy-start | bytes 772
  85.2 55.5 %all-to-all-start = ((bf16[8,4,128,512]{2,3,1,0:T(8,128)(2,1)}), bf16[8,4,128,512]{2,3,1,0:T(8,128)(2,1)}, u32[]{:S(2)}, u32[]{:S(2)}) async-start(bf16[8,4,128,512]{2,3,1,0:T(8,128)(2,1)} %bitcast.48), calls=%async_computation | async-start | bytes 8388608 | tf_op jit(solution)/shard_map/all_to_all | solution.py:14
  146.1 33.8 %all-to-all-start.1 = ((bf16[16,128,512]{2,1,0:T(8,128)(2,1)}), bf16[16,128,512]{2,1,0:T(8,128)(2,1)S(1)}, u32[]{:S(2)}, u32[]{:S(2)}) async-start(bf16[16,128,512]{2,1,0:T(8,128)(2,1)} %select_select_fusion), calls=%async_computation.1 | async-start | bytes 4194304 | tf_op jit(solution)/shard_map/all_to_all | solution.py:63
Sparse Core Ops, SparseCore 0:
  9.0 54.5 all-gather.1
where the time goes:
time: 189 us; the launch traced here: 188 us
  waiting for transfers between devices  132 us (70%)
  matrix products  16.4 us (9%)
  between operations  13.4 us (7%)
  starting transfers between devices  12.8 us (7%)
  local copies, waits for them, and re-layouts  6.76 us (4%)
  other arithmetic  6.68 us (4%)
    all_gather x1, waiting for transfers between devices, on_device(): lax.all_gather(vectors, 'row', axis=1, tiled=True)  55.5 us
    all_to_all x1, waiting for transfers between devices, sent_and_summed(): lax.all_to_all(pieces, axis, split_axis=0, concat_axis=0, tiled=True)  48.2 us
    all_to_all x1, waiting for transfers between devices, on_device(): lax.all_to_all(buffer, 'row', split_axis=0, concat_axis=0, tiled=True)  27.7 us
    dot_general x1, matrix products, on_device(): jnp.einsum('ikbr,ikrv->ibv', left_factors, coeffs, preferred_element_type...  16.4 us
    all_to_all x1, starting transfers between devices, sent_and_summed(): lax.all_to_all(pieces, axis, split_axis=0, concat_axis=0, tiled=True)  6.96 us
    all_to_all x1, starting transfers between devices, on_device(): lax.all_to_all(buffer, 'row', split_axis=0, concat_axis=0, tiled=True)  5.83 us
    reshape x1, local copies, waits for them, and re-layouts, split_up(): return jnp.moveaxis(x.reshape(*before, peers, -1, *after), dim, 0)  5.27 us
  transfers between devices with their start and end apart: 3, of which 3 were waited for; matrix products, arithmetic and copies ran while one was open for 1% of the time, Pallas kernels for 0%

commit v1 on v0

--- a/solution.py
+++ b/solution.py
@@ -2,6 +2,13 @@
 import jax.numpy as jnp
 from jax import lax
 from jax.sharding import PartitionSpec as P
+
+
+def gather_over(value, axis, dim):
+    size = lax.axis_size(axis)
+    shards = jnp.stack([value for _ in range(size)])
+    shards = lax.all_to_all(shards, axis, split_axis=0, concat_axis=0)
+    return jnp.concatenate(shards, axis=dim)
 
 
 def split_up(x, dim, peers):
@@ -51,7 +58,7 @@
     products = jnp.einsum(
         "ikbr,kbv->ikrv",
         right_factors,
-        lax.all_gather(vectors, "row", axis=1, tiled=True),
+        gather_over(vectors, "row", 1),
         preferred_element_type=jnp.float32,
     )
     coeffs = masked_coeffs(products, tile_ranks, rank_width)

time: 189 us -> 271 us (1.43)
  waiting for transfers between devices: 132 us -> 199 us
  starting transfers between devices: 12.8 us -> 29.6 us
  between operations: 13.4 us -> 0.05 us
  local copies, waits for them, and re-layouts: 6.76 us -> 19.8 us
    all_to_all x0 -> x1, waiting for transfers between devices: none -> 123 us  [gather_over(): shards = lax.all_to_all(shards, axis, split_axis=0, concat_axis=0)]
    all_gather x1 -> x0, waiting for transfers between devices: 55.5 us -> none  [on_device(): lax.all_gather(vectors, 'row', axis=1, tiled=True)]
    all_to_all x1, starting transfers between devices: 5.83 us -> 15.7 us  [on_device(): lax.all_to_all(buffer, 'row', split_axis=0, concat_axis=0, tiled=True)]
    all_to_all x0 -> x1, local copies, waits for them, and re-layouts: none -> 7.71 us  [gather_over(): shards = lax.all_to_all(shards, axis, split_axis=0, concat_axis=0)]
    all_to_all x0 -> x1, starting transfers between devices: none -> 6.19 us  [gather_over(): shards = lax.all_to_all(shards, axis, split_axis=0, concat_axis=0)]
    another operation x0 -> x1, local copies, waits for them, and re-layouts: none -> 5.3 us  [gather_over(): shards = jnp.stack([value for _ in range(size)])]
  transfers between devices with their start and end apart: 3 -> 3, of which waited for: 3 -> 3; matrix products, arithmetic and copies ran while one was open for 1% -> 0% of each run, Pallas kernels for 0% -> 0%
where the time goes in v1:
time: 271 us; the launch traced here: 270 us
  waiting for transfers between devices  199 us (73%)
  starting transfers between devices  29.6 us (11%)
  local copies, waits for them, and re-layouts  19.8 us (7%)
  matrix products  16.3 us (6%)
  other arithmetic  6 us (2%)
    all_to_all x1, waiting for transfers between devices, gather_over(): shards = lax.all_to_all(shards, axis, split_axis=0, concat_axis=0)  123 us
    all_to_all x1, waiting for transfers between devices, sent_and_summed(): lax.all_to_all(pieces, axis, split_axis=0, concat_axis=0, tiled=True)  48.2 us
    all_to_all x1, waiting for transfers between devices, on_device(): lax.all_to_all(buffer, 'row', split_axis=0, concat_axis=0, tiled=True)  27.7 us
    dot_general x1, matrix products, on_device(): jnp.einsum('ikbr,ikrv->ibv', left_factors, coeffs, preferred_element_type...  16.3 us
    all_to_all x1, starting transfers between devices, on_device(): lax.all_to_all(buffer, 'row', split_axis=0, concat_axis=0, tiled=True)  15.7 us
    all_to_all x1, starting transfers between devices, sent_and_summed(): lax.all_to_all(pieces, axis, split_axis=0, concat_axis=0, tiled=True)  7.72 us
    all_to_all x1, local copies, waits for them, and re-layouts, gather_over(): shards = lax.all_to_all(shards, axis, split_axis=0, concat_axis=0)  7.71 us
    all_to_all x1, starting transfers between devices, gather_over(): shards = lax.all_to_all(shards, axis, split_axis=0, concat_axis=0)  6.19 us
  transfers between devices with their start and end apart: 3, of which 3 were waited for; matrix products, arithmetic and copies ran while one was open for 0% of the time, Pallas kernels for 0%

profile of v1, /device:TPU:25, one launch (start us, length us, event | category | flops | bytes accessed | tf_op | source)
XLA Modules:
  0.0 270.4 jit_solution(16064700066507868688)
XLA Ops:
  0.0 5.3 %stack.2 = bf16[16,8,64,512]{3,2,1,0:T(8,128)(2,1)} broadcast(bf16[8,64,512]{2,1,0:T(8,128)(2,1)} %param.5), dimensions={1,2,3} | broadcast | bytes 8912896 | tf_op jit(solution)/shard_map/stack | solution.py:9
  5.3 0.0 copy-start
  5.3 6.2 %all-to-all-start = ((bf16[16,8,64,512]{3,2,1,0:T(8,128)(2,1)}), bf16[16,8,64,512]{3,2,1,0:T(8,128)(2,1)}, u32[]{:S(2)}, u32[]{:S(2)}) async-start(bf16[16,8,64,512]{3,2,1,0:T(8,128)(2,1)} %stack.2), calls=%async_computation | async-start | bytes 16777216 | tf_op jit(solution)/shard_map/all_to_all | solution.py:10
  11.5 0.0 copy-done
  11.5 0.1 iota_compare_fusion
  11.6 122.7 %all-to-all-done = bf16[16,8,64,512]{3,2,1,0:T(8,128)(2,1)} async-done(((bf16[16,8,64,512]{3,2,1,0:T(8,128)(2,1)}), bf16[16,8,64,512]{3,2,1,0:T(8,128)(2,1)}, u32[]{:S(2)}, u32[]{:S(2)}) %all-to-all-start) | async-done | bytes 8388640 | tf_op jit(solution)/shard_map/all_to_all | solution.py:10
  134.3 7.7 %copy.15 = bf16[16,8,64,512]{3,2,0,1:T(8,128)(2,1)} copy(bf16[16,8,64,512]{3,2,1,0:T(8,128)(2,1)} %all-to-all-done) | data formatting | bytes 16777216 | tf_op jit(solution)/shard_map/all_to_all | solution.py:10
  142.0 16.3 %fusion.3 = bf16[4,64,8,8,128]{4,3,2,1,0:T(8,128)(2,1)} fusion(bf16[4,8,1024,128]{3,2,1,0:T(8,128)(2,1)} %param.7, pred[4,8,128]{2,1,0:T(8,128)(4,1)S(1)} %iota_compare_fusion, bf16[8,1024,512,1]{2,1,0,3:T(8,128)(2,1)} %bitcast.46, bf16[4,8,1024,128]{3,2,1,0:T(8,128)(2,1)} %param.6), kind=kOutput, calls=%fused_computation.6 | convolution fusion | flops 8596226048 | bytes 29364224 | tf_op jit(solution)/shard_map/ikbr,ikrv->ibv/dot_general | solution.py:65
  158.3 0.0 copy-start.1
  158.3 5.3 %copy.26 = bf16[4,64,8,8,128]{4,3,1,0,2:T(8,128)(2,1)} copy(bf16[4,64,8,8,128]{4,3,2,1,0:T(8,128)(2,1)} %fusion.3) | data formatting | bytes 8388608 | tf_op jit(solution)/shard_map/reshape | solution.py:16
  163.6 7.7 %all-to-all-start.1 = ((bf16[8,4,128,512]{2,3,1,0:T(8,128)(2,1)}), bf16[8,4,128,512]{2,3,1,0:T(8,128)(2,1)}, u32[]{:S(2)}, u32[]{:S(2)}) async-start(bf16[8,4,128,512]{2,3,1,0:T(8,128)(2,1)} %bitcast.45), calls=%async_computation.1 | async-start | bytes 8388608 | tf_op jit(solution)/shard_map/all_to_all | solution.py:21
  171.3 0.0 copy-done.1
  171.3 0.1 and_select_fusion.1
  171.4 0.1 select_reduce_fusion
  171.5 0.1 fusion.10
  171.6 48.2 %all-to-all-done.1 = bf16[8,4,128,512]{2,3,1,0:T(8,128)(2,1)} async-done(((bf16[8,4,128,512]{2,3,1,0:T(8,128)(2,1)}), bf16[8,4,128,512]{2,3,1,0:T(8,128)(2,1)}, u32[]{:S(2)}, u32[]{:S(2)}) %all-to-all-start.1) | async-done | bytes 4194336 | tf_op jit(solution)/shard_map/all_to_all | solution.py:21
  219.8 2.9 %reduce_sum.36 = bf16[4,128,512]{1,2,0:T(8,128)(2,1)S(1)} reduce(bf16[8,4,128,512]{2,3,1,0:T(8,128)(2,1)} %all-to-all-done.1, bf16[]{:T(256)} %constant.65.clone.1), dimensions={0}, to_apply=%region_3.4 | reduce | flops 1835008 | bytes 4718594 | tf_op jit(solution)/shard_map/reduce_sum | solution.py:22
  222.7 0.2 copy.19
  222.9 0.7 gather_fusion
  223.6 1.7 select_select_fusion
  225.2 15.7 %all-to-all-start.2 = ((bf16[16,128,512]{2,1,0:T(8,128)(2,1)}), bf16[16,128,512]{2,1,0:T(8,128)(2,1)S(1)}, u32[]{:S(2)}, u32[]{:S(2)}) async-start(bf16[16,128,512]{2,1,0:T(8,128)(2,1)} %select_select_fusion), calls=%async_computation.2 | async-start | bytes 4194304 | tf_op jit(solution)/shard_map/all_to_all | solution.py:70
  241.0 0.2 select_reduce_fusion.1
  241.2 27.7 %all-to-all-done.2 = bf16[16,128,512]{2,1,0:T(8,128)(2,1)S(1)} async-done(((bf16[16,128,512]{2,1,0:T(8,128)(2,1)}), bf16[16,128,512]{2,1,0:T(8,128)(2,1)S(1)}, u32[]{:S(2)}, u32[]{:S(2)}) %all-to-all-start.2) | async-done | bytes 2097184 | tf_op jit(solution)/shard_map/all_to_all | solution.py:70
  268.9 0.6 gather_fusion.1
  269.5 0.9 broadcast_select_fusion
  (7 shorter events, 0.1 us)
Async XLA Ops:
  5.3 6.2 %copy-start = (s32[4,8]{1,0:T(4,128)S(1)}, s32[4,8]{1,0:T(4,128)}, u32[]{:S(2)}) copy-start(s32[4,8]{1,0:T(4,128)} %param.8) | copy-start | bytes 388
  5.3 128.9 %all-to-all-start = ((bf16[16,8,64,512]{3,2,1,0:T(8,128)(2,1)}), bf16[16,8,64,512]{3,2,1,0:T(8,128)(2,1)}, u32[]{:S(2)}, u32[]{:S(2)}) async-start(bf16[16,8,64,512]{3,2,1,0:T(8,128)(2,1)} %stack.2), calls=%async_computation | async-start | bytes 16777216 | tf_op jit(solution)/shard_map/all_to_all | solution.py:10
  158.3 13.1 %copy-start.1 = (s32[64]{0:T(128)S(1)}, s32[64]{0:T(128)}, u32[]{:S(2)}) copy-start(s32[64]{0:T(128)} %param.9) | copy-start | bytes 772
  163.6 56.2 %all-to-all-start.1 = ((bf16[8,4,128,512]{2,3,1,0:T(8,128)(2,1)}), bf16[8,4,128,512]{2,3,1,0:T(8,128)(2,1)}, u32[]{:S(2)}, u32[]{:S(2)}) async-start(bf16[8,4,128,512]{2,3,1,0:T(8,128)(2,1)} %bitcast.45), calls=%async_computation.1 | async-start | bytes 8388608 | tf_op jit(solution)/shard_map/all_to_all | solution.py:21
  225.2 43.7 %all-to-all-start.2 = ((bf16[16,128,512]{2,1,0:T(8,128)(2,1)}), bf16[16,128,512]{2,1,0:T(8,128)(2,1)S(1)}, u32[]{:S(2)}, u32[]{:S(2)}) async-start(bf16[16,128,512]{2,1,0:T(8,128)(2,1)} %select_select_fusion), calls=%async_computation.2 | async-start | bytes 4194304 | tf_op jit(solution)/shard_map/all_to_all | solution.py:70
